TPU v7x, 32 devices: a whole 2x2x4 slice. The times are simulated.
32 devices in a mesh: dp: 8 (over z, x), mp: 4 (over y, core).
Axes of the slice: x: 2, y: 2, z: 4, core: 2. Of those that a mesh axis runs over, the one named last changes fastest.
Arguments:
- media: bfloat16 [64, 256, 1536], P('dp', None, 'mp'), may hold values from -6 to 6
- time_table: bfloat16 [8, 1536], P(None, 'mp'), may hold values from -4 to 4
- doc_images: int32 [16], P('dp'), may hold values from 0 to 8, as said below
- plan: int32 [8, 8], P('dp'), may hold values from -1 to 19, as said below
- latents: bfloat16 [64, 1536], replicated, may hold values from -6 to 6
- queries: bfloat16 [64, 1024], P(None, 'mp'), may hold values from -450 to 450
- key_weight: bfloat16 [1536, 1024], P(None, 'mp'), may hold values from -0.15625 to 0.15625
- value_weight: bfloat16 [1536, 1024], P(None, 'mp'), may hold values from -0.15625 to 0.15625
- out_weight: bfloat16 [1024, 1536], P('mp'), may hold values from -0.1875 to 0.1875
- cotangent: bfloat16 [32, 64, 1536], P('dp', None, 'mp'), may hold values from -6 to 6
Outputs:
- resampled: bfloat16 [32, 64, 1536], P('dp', None, 'mp')
- key_grad: float32 [1536, 1024], P('dp', 'mp')
- value_grad: float32 [1536, 1024], P('dp', 'mp')
Inputs may be any that keep to these rules, and one draw needn't show every extreme that they name: `doc_images`: A device's documents fill its image slots from slot 0 in document order and hold 8 images or fewer together; some document holds exactly 8. `plan`: entry s of device d's row is -1 exactly when slot s holds no image, else k * 4 + w with k from 0 to 4 and d + k a device of dp: the image goes to work slot w of device d + k. Each work slot receives at most one image; a device sends at most one image for each k from 1 to 4; some device sends one for every such k and fills its own 4 work slots.
All inputs are finite; a program needn't handle non-finite values.
Results may differ from a plain program's by a relative error of at most 0.0096.
Values may be sent and summed in bfloat16 or wider, within the bound.
No kernel may reach another device: no remote copies, remote signals or barrier semaphores. Data moves between devices by JAX's collectives and lax.ppermute only.
A program may use at most 64 MiB of HBM per device.

v0:
```python
import jax
import jax.numpy as jnp
from jax import lax
from jax.sharding import PartitionSpec as P

HEAD = 64
norm_epsilon = 1e-05


def from_behind(block, axis, distance):
    devices = range(lax.axis_size(axis))
    route = [(i - distance, i) for i in devices if i - distance in devices]
    return lax.ppermute(block, axis, route)


def layer_norm(rows_in):
    average = jnp.mean(rows_in, axis=-1, keepdims=True)
    centred = rows_in - average
    spread = jnp.mean(centred * centred, axis=-1, keepdims=True)
    return centred * lax.rsqrt(spread + norm_epsilon)


def local(
    media,
    time_table,
    doc_images,
    plan,
    latents,
    queries,
    key_weight,
    value_weight,
    out_weight,
    cotangent,
):
    slot_cap = media.shape[0]
    image_tokens = media.shape[1]
    quarter = media.shape[2]
    work_slots = cotangent.shape[0]
    latent_count = cotangent.shape[1]
    reach_steps = slot_cap - work_slots
    model_width = latents.shape[1]
    inner_dev = queries.shape[1]
    head_count = inner_dev // HEAD
    context_rows = image_tokens + latent_count
    slot_iota = jnp.arange(slot_cap, dtype=jnp.int32)
    doc_ends = jnp.cumsum(doc_images)
    starts = doc_ends - doc_images
    start_of = jnp.max(jnp.where(starts[None, :] <= slot_iota[:, None], starts[None, :], 0), axis=1)
    position = slot_iota - start_of
    position_hot = (position[:, None] == slot_iota[None, :]).astype(jnp.bfloat16)
    time_rows = jnp.dot(position_hot, time_table, preferred_element_type=jnp.float32)
    framed = (media.astype(jnp.float32) + time_rows[:, None, :]).astype(jnp.bfloat16)
    plan_codes = plan[0]
    is_live = plan_codes >= 0
    helper = jnp.where(is_live, plan_codes // work_slots, -1)
    target = jnp.where(is_live, plan_codes % work_slots, -1)
    target_hot = (target[:, None] == jnp.arange(work_slots, dtype=jnp.int32)[None, :]) & is_live[
        :, None
    ]
    local_map = (target_hot & (helper == 0)[:, None]).astype(jnp.bfloat16)
    work_rows = jnp.einsum("sw,std->wtd", local_map, framed, preferred_element_type=jnp.float32)
    alive_slot = jnp.sum(local_map.astype(jnp.float32), axis=0)
    for offset in range(1, reach_steps + 1):
        chosen = (target_hot & (helper == offset)[:, None]).astype(jnp.bfloat16)
        picked = jnp.sum(chosen, axis=1)
        image_block = jnp.einsum(
            "s,std->td", picked, framed, preferred_element_type=jnp.float32
        ).astype(jnp.bfloat16)
        slot_mark = jnp.sum(chosen, axis=0)
        got_block, got_mark = from_behind((image_block, slot_mark), "dp", offset)
        work_rows = (
            work_rows
            + got_mark.astype(jnp.float32)[:, None, None]
            * got_block.astype(jnp.float32)[None, :, :]
        )
        alive_slot = alive_slot + got_mark.astype(jnp.float32)
    work_media = work_rows.astype(jnp.bfloat16)
    values32 = work_media.astype(jnp.float32)
    first_sum = jnp.sum(values32, axis=-1, keepdims=True)
    square_sum = jnp.sum(values32 * values32, axis=-1, keepdims=True)
    first_all, square_all = lax.psum((first_sum, square_sum), "mp")
    average = first_all / model_width
    spread = square_all / model_width - average * average
    normed_part = ((values32 - average) * lax.rsqrt(spread + norm_epsilon)).astype(jnp.bfloat16)
    normed, cot_full = (
        lax.all_gather(normed_part, "mp", axis=2, tiled=True),
        lax.all_gather(cotangent, "mp", axis=2, tiled=True),
    )
    normed_flat = normed.reshape(work_slots * image_tokens, model_width)
    latent_norm = layer_norm(latents.astype(jnp.float32)).astype(jnp.bfloat16)
    media_keys = (
        jnp.dot(normed_flat, key_weight, preferred_element_type=jnp.float32)
        .astype(jnp.bfloat16)
        .reshape(work_slots, image_tokens, inner_dev)
    )
    media_values = (
        jnp.dot(normed_flat, value_weight, preferred_element_type=jnp.float32)
        .astype(jnp.bfloat16)
        .reshape(work_slots, image_tokens, inner_dev)
    )
    latent_keys = jnp.dot(latent_norm, key_weight, preferred_element_type=jnp.float32).astype(
        jnp.bfloat16
    )
    latent_values = jnp.dot(latent_norm, value_weight, preferred_element_type=jnp.float32).astype(
        jnp.bfloat16
    )
    key_rows = jnp.concatenate(
        [media_keys, jnp.broadcast_to(latent_keys[None], (work_slots, latent_count, inner_dev))], 1
    )
    value_rows = jnp.concatenate(
        [
            media_values,
            jnp.broadcast_to(latent_values[None], (work_slots, latent_count, inner_dev)),
        ],
        1,
    )
    key_heads = key_rows.reshape(work_slots, context_rows, head_count, HEAD)
    value_heads = value_rows.reshape(work_slots, context_rows, head_count, HEAD)
    query_heads = queries.reshape(latent_count, head_count, HEAD)
    scores = (
        jnp.einsum("qhe,wkhe->whqk", query_heads, key_heads, preferred_element_type=jnp.float32)
        * 0.125
    )
    attention = jax.nn.softmax(scores, axis=-1)
    attention_b = attention.astype(jnp.bfloat16)
    attended = jnp.einsum(
        "whqk,wkhe->wqhe", attention_b, value_heads, preferred_element_type=jnp.float32
    ).astype(jnp.bfloat16)
    attended_flat = attended.reshape(work_slots * latent_count, inner_dev)
    partial_out = jnp.dot(attended_flat, out_weight, preferred_element_type=jnp.float32).reshape(
        work_slots, latent_count, model_width
    )
    summed_heads = lax.psum_scatter(
        partial_out.astype(jnp.bfloat16), "mp", scatter_dimension=2, tiled=True
    ).astype(jnp.float32)
    latent_part = lax.dynamic_slice_in_dim(
        latents, lax.axis_index("mp") * quarter, quarter, 1
    ).astype(jnp.float32)
    resampled = ((latent_part[None] + summed_heads) * alive_slot[:, None, None]).astype(
        jnp.bfloat16
    )
    cot_live = cot_full * alive_slot.astype(jnp.bfloat16)[:, None, None]
    grad_attended = lax.dot_general(
        cot_live.reshape(work_slots * latent_count, model_width),
        out_weight,
        (((1,), (1,)), ((), ())),
        preferred_element_type=jnp.float32,
    ).astype(jnp.bfloat16)
    grad_heads = grad_attended.reshape(work_slots, latent_count, head_count, HEAD)
    grad_weights = jnp.einsum(
        "wqhe,wkhe->whqk", grad_heads, value_heads, preferred_element_type=jnp.float32
    )
    row_dot = jnp.sum(attention * grad_weights, axis=-1, keepdims=True)
    grad_scores = attention * (grad_weights - row_dot)
    grad_keys = (
        (
            jnp.einsum(
                "whqk,qhe->wkhe",
                grad_scores,
                query_heads.astype(jnp.float32),
                precision=lax.Precision.HIGHEST,
            )
            * 0.125
        )
        .astype(jnp.bfloat16)
        .reshape(work_slots, context_rows, inner_dev)
    )
    grad_values = (
        jnp.einsum("whqk,wqhe->wkhe", attention_b, grad_heads, preferred_element_type=jnp.float32)
        .astype(jnp.bfloat16)
        .reshape(work_slots, context_rows, inner_dev)
    )
    media_grads = jnp.concatenate(
        [grad_keys[:, :image_tokens], grad_values[:, :image_tokens]], 2
    ).reshape(work_slots * image_tokens, 2 * inner_dev)
    latent_grads = jnp.concatenate(
        [
            jnp.sum(grad_keys[:, image_tokens:].astype(jnp.float32), axis=0),
            jnp.sum(grad_values[:, image_tokens:].astype(jnp.float32), axis=0),
        ],
        1,
    )
    latent_norm32 = latent_norm.astype(jnp.float32)
    inverse_slots = 1.0 / (lax.axis_size("dp") * work_slots)
    media_part = lax.dot_general(
        normed_flat, media_grads, (((0,), (0,)), ((), ())), preferred_element_type=jnp.float32
    )
    latent_term = lax.dot_general(
        latent_norm32,
        latent_grads,
        (((0,), (0,)), ((), ())),
        precision=lax.Precision.HIGHEST,
        preferred_element_type=jnp.float32,
    )
    shares = lax.psum_scatter(
        (media_part + latent_term) * inverse_slots, "dp", scatter_dimension=0, tiled=True
    )
    return (resampled, shares[:, :inner_dev], shares[:, inner_dev:])


def solution(mesh):
    return jax.shard_map(
        local,
        mesh=mesh,
        in_specs=(
            P("dp", None, "mp"),
            P(None, "mp"),
            P("dp"),
            P("dp", None),
            P(),
            P(None, "mp"),
            P(None, "mp"),
            P(None, "mp"),
            P("mp", None),
            P("dp", None, "mp"),
        ),
        out_specs=(P("dp", None, "mp"), P("dp", "mp"), P("dp", "mp")),
        check_vma=False,
    )
```

profile of v0, /device:TPU:0, one launch (start us, length us, event | category | flops | bytes accessed | tf_op | source)
XLA Modules:
  0.0 241.2 jit_solution(2323015476926273709)
XLA Ops:
  11.1 1.7 add_convert_fusion
  14.2 4.9 %collective-permute-start.1 = (bf16[256,384]{1,0:T(8,128)(2,1)S(1)}, bf16[256,384]{1,0:T(8,128)(2,1)S(1)}, u32[]{:S(2)}, u32[]{:S(2)}) collective-permute-start(bf16[256,384]{1,0:T(8,128)(2,1)S(1)} %bitcast.118), channel_id=1, source_target_pairs={{0,4},{4,8},{8,12},{12,16},{16,20},{20,24},{24,28},{1,5},{5,9},{9,... | collective-permute-start | bytes 589832 | tf_op jit(solution)/shard_map/ppermute | solution.py:13
  20.2 3.5 %collective-permute-start.3 = (bf16[256,384]{1,0:T(8,128)(2,1)S(1)}, bf16[256,384]{1,0:T(8,128)(2,1)S(1)}, u32[]{:S(2)}, u32[]{:S(2)}) collective-permute-start(bf16[256,384]{1,0:T(8,128)(2,1)S(1)} %bitcast.119), channel_id=1, source_target_pairs={{0,8},{4,12},{8,16},{12,20},{16,24},{20,28},{1,9},{5,13},{9,17},{1... | collective-permute-start | bytes 589832 | tf_op jit(solution)/shard_map/ppermute | solution.py:13
  24.8 4.5 %collective-permute-start.5 = (bf16[256,384]{1,0:T(8,128)(2,1)S(1)}, bf16[256,384]{1,0:T(8,128)(2,1)S(1)}, u32[]{:S(2)}, u32[]{:S(2)}) collective-permute-start(bf16[256,384]{1,0:T(8,128)(2,1)S(1)} %bitcast.120), channel_id=1, source_target_pairs={{0,12},{4,16},{8,20},{12,24},{16,28},{1,13},{5,17},{9,21},{13,25},... | collective-permute-start | bytes 589832 | tf_op jit(solution)/shard_map/ppermute | solution.py:13
  30.4 1.9 collective-permute-start.7
  32.4 2.7 %collective-permute-start = (bf16[4]{0:T(256)(128)(2,1)S(1)}, bf16[4]{0:T(256)(128)(2,1)S(1)}, u32[]{:S(2)}, u32[]{:S(2)}) collective-permute-start(bf16[4]{0:T(256)(128)(2,1)S(1)} %get-tuple-element.5), channel_id=1, source_target_pairs={{0,4},{4,8},{8,12},{12,16},{16,20},{20,24},{24,28},{1,5},{5,9},{9,... | collective-permute-start | bytes 32 | tf_op jit(solution)/shard_map/ppermute | solution.py:13
  36.4 14.4 %collective-permute-start.6 = (bf16[4]{0:T(256)(128)(2,1)S(1)}, bf16[4]{0:T(256)(128)(2,1)S(1)}, u32[]{:S(2)}, u32[]{:S(2)}) collective-permute-start(bf16[4]{0:T(256)(128)(2,1)S(1)} %get-tuple-element.14), channel_id=1, source_target_pairs={{0,16},{4,20},{8,24},{12,28},{1,17},{5,21},{9,25},{13,29},{2,18},{... | collective-permute-start | bytes 32 | tf_op jit(solution)/shard_map/ppermute | solution.py:13
  57.4 3.6 %convert_reduce_fusion = (f32[4,256]{0,1:T(8,128)S(1)}, f32[4,256]{0,1:T(8,128)S(1)}, bf16[4,256,384]{2,0,1:T(4,128)(2,1)S(1)}) fusion(f32[256,384]{1,0:T(8,128)S(1)} %convert_element_type.173, f32[4]{0:T(128)S(1)} %convert_element_type.171, f32[256,384]{1,0:T(8,128)S(1)} %convert_element_type.169, f32[4]{0:T(128)S(1)} %convert_element_type.167, ...), kind=kOutput, calls=%fused_computation.8 | convolution fusion | flops 11401248 | bytes 3940456 | tf_op jit(solution)/shard_map/sw,std->wtd/dot_general | solution.py:61
  61.1 12.9 %all-reduce = (f32[4,256,1]{0,1,2:T(8,128)S(1)}, f32[4,256,1]{0,1,2:T(8,128)S(1)}) all-reduce(f32[4,256,1]{0,1,2:T(8,128)S(1)} %bitcast.123, f32[4,256,1]{0,1,2:T(8,128)S(1)} %bitcast.122), channel_id=1, replica_groups=mesh['dp'=8,'mp'=4] {'mp'}, use_global_device_ids=true, to_apply=%region_13.14 | all-reduce | flops 2048 | bytes 16384 | tf_op jit(solution)/shard_map/psum | solution.py:81
  77.3 9.5 %all_gather.7 = bf16[4,64,1536]{2,1,0:T(8,128)(2,1)S(1)} all-gather(bf16[4,64,384]{2,1,0:T(8,128)(2,1)S(1)} %copy-done.8), channel_id=1, replica_groups=mesh['dp'=8,'mp'=4] {'mp'}, dimensions={2}, use_global_device_ids=true | all-gather | bytes 983040 | tf_op jit(solution)/shard_map/all_gather | solution.py:87
  87.6 25.2 %all-gather.2.cloned.1.call-done = bf16[4,256,1536]{2,0,1:T(4,128)(2,1)} async-done(((bf16[4,256,384]{2,0,1:T(4,128)(2,1)}), bf16[4,256,1536]{2,0,1:T(4,128)(2,1)}) %all-gather.2.cloned.1.call-update) | async-done | bytes 3145744 | tf_op jit(solution)/shard_map/all_gather | solution.py:86
  112.8 2.5 %copy.72 = bf16[4,256,1536]{2,1,0:T(8,128)(2,1)S(1)} copy(bf16[4,256,1536]{2,0,1:T(4,128)(2,1)} %all-gather.2.cloned.1.call-done) | data formatting | bytes 6291456 | tf_op jit(solution)/shard_map/all_gather | solution.py:86
  115.3 1.8 convolution_convert_fusion.2
  117.0 1.8 convolution_convert_fusion.3
  118.8 2.1 reshape.235
  122.6 1.8 fusion.95
  124.5 3.0 %multiply_reduce_fusion = (f32[4,4,64]{2,0,1:T(4,128)S(1)}, bf16[4,4,64,320]{3,2,0,1:T(8,128)(2,1)S(1)}, f32[4,4,64,320]{3,2,0,1:T(8,128)}) fusion(f32[4,4,64,320]{3,2,0,1:T(8,128)} %get-tuple-element.40, f32[4,4,64]{2,0,1:T(4,128)S(1)} %get-tuple-element.39, bf16[4,64,4,64]{3,2,1,0:T(4,128)(2,1)S(1)} %reshape.219, ...), kind=kOutput, calls=%fused_computation.19 | convolution fusion | flops 44563456 | bytes 4071424 | tf_op jit(solution)/shard_map/wqhe,wkhe->whqk/dot_general | solution.py:150
  129.8 1.7 reshape.237
  131.8 3.1 %fusion.15 = bf16[4,320,4,64]{1,3,0,2:T(8,128)(2,1)S(1)} fusion(bf16[64,4,64,1]{0,2,3,1:T(8,128)(2,1)S(1)} %copy.101, f32[4,4,64,320]{3,2,0,1:T(8,128)} %get-tuple-element.41, f32[4,4,64]{2,0,1:T(4,128)S(1)} %get-tuple-element.27, f32[4,4,64,320]{3,2,0,1:T(8,128)} %get-tuple-element.40, f32[4,4,64]{2,0,1:T(4,128)S(1)} %get-tuple-element.39), kind=kOutput, calls=%fused_computation.24 | convolution fusion | flops 253296640 | bytes 3317760 | tf_op jit(solution)/shard_map/whqk,qhe->wkhe/dot_general | solution.py:157
  138.9 4.2 %convolution_bitcast_fusion = f32[1536,512]{1,0:T(8,128)S(1)} fusion(bf16[4,256,256]{2,1,0:T(8,128)(2,1)} %copy.116, bf16[4,256,256]{2,1,0:T(8,128)(2,1)} %copy.115, bf16[4,256,1536]{2,0,1:T(4,128)(2,1)} %all-gather.2.cloned.1.call-done), kind=kOutput, calls=%fused_computation.3 | convolution fusion | flops 1612709888 | bytes 7340032 | tf_op jit(solution)/shard_map/dot_general | solution.py:185
  143.1 3.3 %fusion.1 = f32[1536,512]{1,0:T(8,128)} fusion(f32[1536,512]{1,0:T(8,128)S(1)} %convolution_bitcast_fusion, f32[64,256]{0,1:T(8,128)S(1)} %get-tuple-element.42, f32[64,256]{0,1:T(8,128)S(1)} %get-tuple-element.43, bf16[64,1536]{1,0:T(8,128)(2,1)S(1)} %copy-done.1, f32[64]{0:T(128)S(1)} %add_rsqrt_fusion, f32[64]{0:T(128)S(1)} %broadcast_multiply_fusion.1), kind=kOutput, calls=%fused_computation.2 | convolution fusion | flops 605978624 | bytes 6619648 | tf_op jit(solution)/shard_map/dot_general | solution.py:188
  146.5 8.5 %reduce-scatter.7.cloned.1.call-done = bf16[384,256]{1,0:T(8,128)(2,1)} async-done(((bf16[1536,256]{1,0:T(8,128)(2,1)}), bf16[384,256]{1,0:T(8,128)(2,1)}) %reduce-scatter.7.cloned.1.call-update) | async-done | bytes 196624
  157.1 75.8 %reduce-scatter.5.cloned.1.call-done = f32[192,512]{1,0:T(8,128)} async-done(((f32[1536,512]{1,0:T(8,128)}), f32[192,512]{1,0:T(8,128)}) %reduce-scatter.5.cloned.1.call-update) | async-done | bytes 393232 | tf_op jit(solution)/shard_map/reduce_scatter | solution.py:195
  232.9 1.8 fusion.94
  (113 shorter events, 30.6 us)
Async XLA Ops:
  7.2 79.8 %copy-start = (bf16[256,1536]{1,0:T(8,128)(2,1)S(1)}, bf16[256,1536]{1,0:T(8,128)(2,1)}, u32[]{:S(2)}) copy-start(bf16[256,1536]{1,0:T(8,128)(2,1)} %param.18) | copy-start | bytes 2359300
  7.2 105.6 %all-gather.2.cloned.1.call-start = ((), (), s32[]{:S(2)}) async-start(), calls=%async_computation.2 | async-start | bytes 3932160 | tf_op jit(solution)/shard_map/all_gather | solution.py:86
  14.2 43.0 %collective-permute-start.1 = (bf16[256,384]{1,0:T(8,128)(2,1)S(1)}, bf16[256,384]{1,0:T(8,128)(2,1)S(1)}, u32[]{:S(2)}, u32[]{:S(2)}) collective-permute-start(bf16[256,384]{1,0:T(8,128)(2,1)S(1)} %bitcast.118), channel_id=1, source_target_pairs={{0,4},{4,8},{8,12},{12,16},{16,20},{20,24},{24,28},{1,5},{5,9},{9,... | collective-permute-start | bytes 589832 | tf_op jit(solution)/shard_map/ppermute | solution.py:13
  20.2 37.1 %collective-permute-start.3 = (bf16[256,384]{1,0:T(8,128)(2,1)S(1)}, bf16[256,384]{1,0:T(8,128)(2,1)S(1)}, u32[]{:S(2)}, u32[]{:S(2)}) collective-permute-start(bf16[256,384]{1,0:T(8,128)(2,1)S(1)} %bitcast.119), channel_id=1, source_target_pairs={{0,8},{4,12},{8,16},{12,20},{16,24},{20,28},{1,9},{5,13},{9,17},{1... | collective-permute-start | bytes 589832 | tf_op jit(solution)/shard_map/ppermute | solution.py:13
  24.8 32.5 %collective-permute-start.5 = (bf16[256,384]{1,0:T(8,128)(2,1)S(1)}, bf16[256,384]{1,0:T(8,128)(2,1)S(1)}, u32[]{:S(2)}, u32[]{:S(2)}) collective-permute-start(bf16[256,384]{1,0:T(8,128)(2,1)S(1)} %bitcast.120), channel_id=1, source_target_pairs={{0,12},{4,16},{8,20},{12,24},{16,28},{1,13},{5,17},{9,21},{13,25},... | collective-permute-start | bytes 589832 | tf_op jit(solution)/shard_map/ppermute | solution.py:13
  30.4 26.9 %collective-permute-start.7 = (bf16[256,384]{1,0:T(8,128)(2,1)S(1)}, bf16[256,384]{1,0:T(8,128)(2,1)S(1)}, u32[]{:S(2)}, u32[]{:S(2)}) collective-permute-start(bf16[256,384]{1,0:T(8,128)(2,1)S(1)} %bitcast.121), channel_id=1, source_target_pairs={{0,16},{4,20},{8,24},{12,28},{1,17},{5,21},{9,25},{13,29},{2,18},{... | collective-permute-start | bytes 589832 | tf_op jit(solution)/shard_map/ppermute | solution.py:13
  32.4 4.0 %collective-permute-start = (bf16[4]{0:T(256)(128)(2,1)S(1)}, bf16[4]{0:T(256)(128)(2,1)S(1)}, u32[]{:S(2)}, u32[]{:S(2)}) collective-permute-start(bf16[4]{0:T(256)(128)(2,1)S(1)} %get-tuple-element.5), channel_id=1, source_target_pairs={{0,4},{4,8},{8,12},{12,16},{16,20},{20,24},{24,28},{1,5},{5,9},{9,... | collective-permute-start | bytes 32 | tf_op jit(solution)/shard_map/ppermute | solution.py:13
  36.4 24.6 %copy-start.10 = (bf16[4]{0:T(256)(128)(2,1)}, bf16[4]{0:T(256)(128)(2,1)S(1)}, u32[]{:S(2)}) copy-start(bf16[4]{0:T(256)(128)(2,1)S(1)} %collective-permute-done) | copy-start | bytes 28
  36.4 15.7 %collective-permute-start.6 = (bf16[4]{0:T(256)(128)(2,1)S(1)}, bf16[4]{0:T(256)(128)(2,1)S(1)}, u32[]{:S(2)}, u32[]{:S(2)}) collective-permute-start(bf16[4]{0:T(256)(128)(2,1)S(1)} %get-tuple-element.14), channel_id=1, source_target_pairs={{0,16},{4,20},{8,24},{12,28},{1,17},{5,21},{9,25},{13,29},{2,18},{... | collective-permute-start | bytes 32 | tf_op jit(solution)/shard_map/ppermute | solution.py:13
  52.1 8.9 %copy-start.12 = (bf16[4]{0:T(256)(128)(2,1)}, bf16[4]{0:T(256)(128)(2,1)S(1)}, u32[]{:S(2)}) copy-start(bf16[4]{0:T(256)(128)(2,1)S(1)} %collective-permute-done.6) | copy-start | bytes 28
  52.1 2.6 %collective-permute-start.4 = (bf16[4]{0:T(256)(128)(2,1)S(1)}, bf16[4]{0:T(256)(128)(2,1)S(1)}, u32[]{:S(2)}, u32[]{:S(2)}) collective-permute-start(bf16[4]{0:T(256)(128)(2,1)S(1)} %get-tuple-element.16), channel_id=1, source_target_pairs={{0,12},{4,16},{8,20},{12,24},{16,28},{1,13},{5,17},{9,21},{13,25},... | collective-permute-start | bytes 32 | tf_op jit(solution)/shard_map/ppermute | solution.py:13
  54.7 6.4 %copy-start.14 = (bf16[4]{0:T(256)(128)(2,1)}, bf16[4]{0:T(256)(128)(2,1)S(1)}, u32[]{:S(2)}) copy-start(bf16[4]{0:T(256)(128)(2,1)S(1)} %collective-permute-done.4) | copy-start | bytes 28
  54.7 2.6 %collective-permute-start.2 = (bf16[4]{0:T(256)(128)(2,1)S(1)}, bf16[4]{0:T(256)(128)(2,1)S(1)}, u32[]{:S(2)}, u32[]{:S(2)}) collective-permute-start(bf16[4]{0:T(256)(128)(2,1)S(1)} %get-tuple-element.18), channel_id=1, source_target_pairs={{0,8},{4,12},{8,16},{12,20},{16,24},{20,28},{1,9},{5,13},{9,17},{1... | collective-permute-start | bytes 32 | tf_op jit(solution)/shard_map/ppermute | solution.py:13
  57.2 3.8 %copy-start.16 = (bf16[4]{0:T(256)(128)(2,1)}, bf16[4]{0:T(256)(128)(2,1)S(1)}, u32[]{:S(2)}) copy-start(bf16[4]{0:T(256)(128)(2,1)S(1)} %collective-permute-done.2) | copy-start | bytes 28
  74.0 1.9 copy-start.5
  75.5 1.8 copy-start.8
  75.5 79.4 %reduce-scatter.7.cloned.1.call-start = ((), (), s32[]{:S(2)}) async-start(), calls=%async_computation.4 | async-start | bytes 983040
  76.0 10.9 %copy-start.11 = (bf16[4]{0:T(256)(128)(2,1)S(1)}, bf16[4]{0:T(256)(128)(2,1)}, u32[]{:S(2)}) copy-start(bf16[4]{0:T(256)(128)(2,1)} %copy-done.10) | copy-start | bytes 28
  76.0 10.8 %copy-start.13 = (bf16[4]{0:T(256)(128)(2,1)S(1)}, bf16[4]{0:T(256)(128)(2,1)}, u32[]{:S(2)}) copy-start(bf16[4]{0:T(256)(128)(2,1)} %copy-done.12) | copy-start | bytes 28
  76.0 10.8 %copy-start.15 = (bf16[4]{0:T(256)(128)(2,1)S(1)}, bf16[4]{0:T(256)(128)(2,1)}, u32[]{:S(2)}) copy-start(bf16[4]{0:T(256)(128)(2,1)} %copy-done.14) | copy-start | bytes 28
  76.0 10.8 %copy-start.17 = (bf16[4]{0:T(256)(128)(2,1)S(1)}, bf16[4]{0:T(256)(128)(2,1)}, u32[]{:S(2)}) copy-start(bf16[4]{0:T(256)(128)(2,1)} %copy-done.16) | copy-start | bytes 28
  87.6 36.9 %copy-start.2 = (bf16[4,64,4,64]{3,2,1,0:T(4,128)(2,1)}, bf16[4,64,4,64]{3,2,1,0:T(4,128)(2,1)S(1)}, u32[]{:S(2)}) copy-start(bf16[4,64,4,64]{3,2,1,0:T(4,128)(2,1)S(1)} %reshape.219) | copy-start | bytes 393220
  118.8 2.6 %copy-start.7 = (bf16[1024,256]{1,0:T(8,128)(2,1)S(1)}, bf16[1024,256]{1,0:T(8,128)(2,1)}, u32[]{:S(2)}) copy-start(bf16[1024,256]{1,0:T(8,128)(2,1)} %convolution_convert_fusion.2) | copy-start | bytes 1572868
  131.5 101.4 %reduce-scatter.5.cloned.1.call-start = ((), (), s32[]{:S(2)}) async-start(), calls=%async_computation.3 | async-start | bytes 3538944 | tf_op jit(solution)/shard_map/reduce_scatter | solution.py:195
  (5 other events, 6.3 us)
Sparse Core Ops, SparseCore 0:
  75.6 37.1 all-gather.1
  131.6 23.2 reduce-scatter.6
  158.5 74.3 reduce-scatter.4
where the time goes:
time: 242 us; the launch traced here: 241 us
  waiting for transfers between devices  115 us (48%)
  starting transfers between devices  34.8 us (14%)
  matrix products  31.2 us (13%)
  blocking collectives  22.4 us (9%)
  local copies, waits for them, and re-layouts  15.8 us (7%)
  between operations  14.3 us (6%)
  other arithmetic  7.98 us (3%)
    reduce_scatter x1, waiting for transfers between devices, local(): lax.psum_scatter((media_part + latent_term) * inverse_slots, 'dp', scatte...  75.8 us
    ppermute x8, starting transfers between devices, from_behind(): return lax.ppermute(block, axis, route)  34.5 us
    all_gather x1, waiting for transfers between devices, local(): lax.all_gather(normed_part, 'mp', axis=2, tiled=True)  25.2 us
    psum x1, blocking collectives, local(): first_all, square_all = lax.psum((first_sum, square_sum), 'mp')  12.9 us
    all_gather x1, blocking collectives, local(): lax.all_gather(cotangent, 'mp', axis=2, tiled=True)  9.53 us
    unnamed x4, waiting for transfers between devices  8.5 us
    unnamed x42, local copies, waits for them, and re-layouts  6.93 us
    ppermute x8, waiting for transfers between devices, from_behind(): return lax.ppermute(block, axis, route)  5.09 us
  transfers between devices with their start and end apart: 11, of which 7 were waited for; matrix products, arithmetic and copies ran while one was open for 9% of the time, Pallas kernels for 0%

commit v1 on v0

--- a/solution.py
+++ b/solution.py
@@ -83,7 +83,9 @@
     spread = square_all / model_width - average * average
     normed_part = ((values32 - average) * lax.rsqrt(spread + norm_epsilon)).astype(jnp.bfloat16)
     normed, cot_full = (
-        lax.all_gather(normed_part, "mp", axis=2, tiled=True),
+        jnp.concatenate(
+            lax.all_to_all(jnp.stack([normed_part] * lax.axis_size("mp")), "mp", 0, 0), axis=2
+        ),
         lax.all_gather(cotangent, "mp", axis=2, tiled=True),
     )
     normed_flat = normed.reshape(work_slots * image_tokens, model_width)

time: 242 us -> 261 us (1.079)
  blocking collectives: 22.4 us -> 53.4 us
  waiting for transfers between devices: 115 us -> 95.5 us
  starting transfers between devices: 34.8 us -> 39.5 us
  local copies, waits for them, and re-layouts: 15.8 us -> 20 us
    all_gather x1, blocking collectives: 9.53 us -> 40.5 us  [local(): lax.all_gather(cotangent, 'mp', axis=2, tiled=True)]
    all_gather x1 -> x0, waiting for transfers between devices: 25.2 us -> none  [local(): lax.all_gather(normed_part, 'mp', axis=2, tiled=True)]
    unnamed x4 -> x3, waiting for transfers between devices: 8.5 us -> 14.6 us
    all_to_all x0 -> x1, starting transfers between devices: none -> 4.77 us  [local(): lax.all_to_all(jnp.stack([normed_part] * lax.axis_size('mp')), 'mp', 0, 0)]
    reshape x0 -> x1, local copies, waits for them, and re-layouts: none -> 4.41 us  [local(): jnp.concatenate(lax.all_to_all(jnp.stack([normed_part] * lax.axis_size('m...]
    unnamed x42 -> x31, local copies, waits for them, and re-layouts: 6.93 us -> 7.25 us
  transfers between devices with their start and end apart: 11 -> 11, of which waited for: 7 -> 6; matrix products, arithmetic and copies ran while one was open for 9% -> 8% of each run, Pallas kernels for 0% -> 0%
where the time goes in v1:
time: 261 us; the launch traced here: 260 us
  waiting for transfers between devices  95.5 us (37%)
  blocking collectives  53.4 us (20%)
  starting transfers between devices  39.5 us (15%)
  matrix products  29 us (11%)
  local copies, waits for them, and re-layouts  20 us (8%)
  between operations  14.7 us (6%)
  other arithmetic  8.29 us (3%)
    reduce_scatter x1, waiting for transfers between devices, local(): lax.psum_scatter((media_part + latent_term) * inverse_slots, 'dp', scatte...  76 us
    all_gather x1, blocking collectives, local(): lax.all_gather(cotangent, 'mp', axis=2, tiled=True)  40.5 us
    ppermute x8, starting transfers between devices, from_behind(): return lax.ppermute(block, axis, route)  34.5 us
    unnamed x3, waiting for transfers between devices  14.6 us
    psum x1, blocking collectives, local(): first_all, square_all = lax.psum((first_sum, square_sum), 'mp')  12.9 us
    unnamed x31, local copies, waits for them, and re-layouts  7.25 us
  transfers between devices with their start and end apart: 11, of which 6 were waited for; matrix products, arithmetic and copies ran while one was open for 8% of the time, Pallas kernels for 0%

profile of v1, /device:TPU:0, one launch (start us, length us, event | category | flops | bytes accessed | tf_op | source)
XLA Modules:
  0.0 260.4 jit_solution(2062857427746339927)
XLA Ops:
  11.1 1.7 add_convert_fusion
  14.2 4.9 %collective-permute-start.1 = (bf16[256,384]{1,0:T(8,128)(2,1)S(1)}, bf16[256,384]{1,0:T(8,128)(2,1)S(1)}, u32[]{:S(2)}, u32[]{:S(2)}) collective-permute-start(bf16[256,384]{1,0:T(8,128)(2,1)S(1)} %bitcast.125), channel_id=1, source_target_pairs={{0,4},{4,8},{8,12},{12,16},{16,20},{20,24},{24,28},{1,5},{5,9},{9,... | collective-permute-start | bytes 589832 | tf_op jit(solution)/shard_map/ppermute | solution.py:13
  20.2 3.5 %collective-permute-start.3 = (bf16[256,384]{1,0:T(8,128)(2,1)S(1)}, bf16[256,384]{1,0:T(8,128)(2,1)S(1)}, u32[]{:S(2)}, u32[]{:S(2)}) collective-permute-start(bf16[256,384]{1,0:T(8,128)(2,1)S(1)} %bitcast.126), channel_id=1, source_target_pairs={{0,8},{4,12},{8,16},{12,20},{16,24},{20,28},{1,9},{5,13},{9,17},{1... | collective-permute-start | bytes 589832 | tf_op jit(solution)/shard_map/ppermute | solution.py:13
  24.8 4.6 %collective-permute-start.5 = (bf16[256,384]{1,0:T(8,128)(2,1)S(1)}, bf16[256,384]{1,0:T(8,128)(2,1)S(1)}, u32[]{:S(2)}, u32[]{:S(2)}) collective-permute-start(bf16[256,384]{1,0:T(8,128)(2,1)S(1)} %bitcast.127), channel_id=1, source_target_pairs={{0,12},{4,16},{8,20},{12,24},{16,28},{1,13},{5,17},{9,21},{13,25},... | collective-permute-start | bytes 589832 | tf_op jit(solution)/shard_map/ppermute | solution.py:13
  30.5 1.9 collective-permute-start.7
  32.5 2.7 %collective-permute-start = (bf16[4]{0:T(256)(128)(2,1)S(1)}, bf16[4]{0:T(256)(128)(2,1)S(1)}, u32[]{:S(2)}, u32[]{:S(2)}) collective-permute-start(bf16[4]{0:T(256)(128)(2,1)S(1)} %get-tuple-element.5), channel_id=1, source_target_pairs={{0,4},{4,8},{8,12},{12,16},{16,20},{20,24},{24,28},{1,5},{5,9},{9,... | collective-permute-start | bytes 32 | tf_op jit(solution)/shard_map/ppermute | solution.py:13
  36.5 14.3 %collective-permute-start.6 = (bf16[4]{0:T(256)(128)(2,1)S(1)}, bf16[4]{0:T(256)(128)(2,1)S(1)}, u32[]{:S(2)}, u32[]{:S(2)}) collective-permute-start(bf16[4]{0:T(256)(128)(2,1)S(1)} %get-tuple-element.14), channel_id=1, source_target_pairs={{0,16},{4,20},{8,24},{12,28},{1,17},{5,21},{9,25},{13,29},{2,18},{... | collective-permute-start | bytes 32 | tf_op jit(solution)/shard_map/ppermute | solution.py:13
  57.4 3.6 %convert_reduce_fusion = (f32[4,256]{0,1:T(8,128)S(1)}, f32[4,256]{0,1:T(8,128)S(1)}, bf16[4,256,384]{2,0,1:T(4,128)(2,1)S(1)}) fusion(f32[256,384]{1,0:T(8,128)S(1)} %convert_element_type.173, f32[4]{0:T(128)S(1)} %convert_element_type.171, f32[256,384]{1,0:T(8,128)S(1)} %convert_element_type.169, f32[4]{0:T(128)S(1)} %convert_element_type.167, ...), kind=kOutput, calls=%fused_computation.7 | convolution fusion | flops 11401248 | bytes 3940456 | tf_op jit(solution)/shard_map/sw,std->wtd/dot_general | solution.py:61
  61.0 12.9 %all-reduce = (f32[4,256,1]{0,1,2:T(8,128)S(1)}, f32[4,256,1]{0,1,2:T(8,128)S(1)}) all-reduce(f32[4,256,1]{0,1,2:T(8,128)S(1)} %bitcast.130, f32[4,256,1]{0,1,2:T(8,128)S(1)} %bitcast.129), channel_id=1, replica_groups=mesh['dp'=8,'mp'=4] {'mp'}, use_global_device_ids=true, to_apply=%region_13.14 | all-reduce | flops 2048 | bytes 16384 | tf_op jit(solution)/shard_map/psum | solution.py:81
  74.8 2.1 stack.2
  76.9 4.8 %all-to-all-start = ((bf16[4,4,256,384]{3,2,1,0:T(8,128)(2,1)}), bf16[4,4,256,384]{3,2,1,0:T(8,128)(2,1)}, u32[]{:S(2)}, u32[]{:S(2)}) async-start(bf16[4,4,256,384]{3,2,1,0:T(8,128)(2,1)} %stack.2), calls=%async_computation | async-start | bytes 6291456 | tf_op jit(solution)/shard_map/all_to_all | solution.py:87
  83.1 40.5 %all_gather.3 = bf16[4,64,1536]{2,1,0:T(8,128)(2,1)S(1)} all-gather(bf16[4,64,384]{2,1,0:T(8,128)(2,1)S(1)} %copy-done.11), channel_id=1, replica_groups=mesh['dp'=8,'mp'=4] {'mp'}, dimensions={2}, use_global_device_ids=true | all-gather | bytes 983040 | tf_op jit(solution)/shard_map/all_gather | solution.py:89
  124.4 4.4 %copy.69 = bf16[4,256,4,384]{3,2,1,0:T(4,128)(2,1)S(1)} copy(bf16[4,256,4,384]{3,1,0,2:T(8,128)(2,1)} %bitcast.16) | data formatting | bytes 6291456 | tf_op jit(solution)/shard_map/reshape | solution.py:86
  131.0 1.8 convolution_convert_fusion.3
  134.8 1.8 fusion.90
  136.7 3.0 %multiply_reduce_fusion = (f32[4,4,64]{2,0,1:T(4,128)S(1)}, bf16[4,4,64,320]{3,2,0,1:T(8,128)(2,1)S(1)}, f32[4,4,64,320]{3,2,0,1:T(8,128)}) fusion(f32[4,4,64,320]{3,2,0,1:T(8,128)} %get-tuple-element.40, f32[4,4,64]{2,0,1:T(4,128)S(1)} %get-tuple-element.39, bf16[4,64,4,64]{3,2,1,0:T(4,128)(2,1)S(1)} %reshape.223, ...), kind=kOutput, calls=%fused_computation.18 | convolution fusion | flops 44563456 | bytes 4071424 | tf_op jit(solution)/shard_map/wqhe,wkhe->whqk/dot_general | solution.py:152
  142.0 1.7 reshape.241
  144.0 3.1 %fusion.15 = bf16[4,320,4,64]{1,3,0,2:T(8,128)(2,1)S(1)} fusion(bf16[64,4,64,1]{0,2,3,1:T(8,128)(2,1)S(1)} %copy.96, f32[4,4,64,320]{3,2,0,1:T(8,128)} %get-tuple-element.41, f32[4,4,64]{2,0,1:T(4,128)S(1)} %get-tuple-element.27, f32[4,4,64,320]{3,2,0,1:T(8,128)} %get-tuple-element.40, f32[4,4,64]{2,0,1:T(4,128)S(1)} %get-tuple-element.39), kind=kOutput, calls=%fused_computation.23 | convolution fusion | flops 253296640 | bytes 3317760 | tf_op jit(solution)/shard_map/whqk,qhe->wkhe/dot_general | solution.py:159
  149.2 1.3 copy.86
  151.7 4.0 %fusion.93 = f32[1536,512]{1,0:T(8,128)S(1)} fusion(bf16[1024,1536]{1,0:T(8,128)(2,1)} %bitcast.115, bf16[1024,512]{1,0:T(8,128)(2,1)} %bitcast.120), kind=kOutput, calls=%fused_computation.129 | convolution fusion | flops 1610612736 | bytes 7340032 | tf_op jit(solution)/shard_map/dot_general | solution.py:187
  155.7 3.3 %fusion.1 = f32[1536,512]{1,0:T(8,128)} fusion(f32[1536,512]{1,0:T(8,128)S(1)} %fusion.93, f32[64,256]{0,1:T(8,128)S(1)} %get-tuple-element.42, f32[64,256]{0,1:T(8,128)S(1)} %get-tuple-element.43, bf16[64,1536]{1,0:T(8,128)(2,1)S(1)} %copy-done.1, f32[64]{0:T(128)S(1)} %add_rsqrt_fusion, f32[64]{0:T(128)S(1)} %broadcast_multiply_fusion.1), kind=kOutput, calls=%fused_computation.2 | convolution fusion | flops 605978624 | bytes 6619648 | tf_op jit(solution)/shard_map/dot_general | solution.py:190
  159.1 14.5 %reduce-scatter.7.cloned.1.call-done = bf16[384,256]{1,0:T(8,128)(2,1)} async-done(((bf16[1536,256]{1,0:T(8,128)(2,1)}), bf16[384,256]{1,0:T(8,128)(2,1)}) %reduce-scatter.7.cloned.1.call-update) | async-done | bytes 196624
  175.8 76.0 %reduce-scatter.5.cloned.1.call-done = f32[192,512]{1,0:T(8,128)} async-done(((f32[1536,512]{1,0:T(8,128)}), f32[192,512]{1,0:T(8,128)}) %reduce-scatter.5.cloned.1.call-update) | async-done | bytes 393232 | tf_op jit(solution)/shard_map/reduce_scatter | solution.py:197
  251.8 1.8 fusion.89
  (105 shorter events, 31.4 us)
Async XLA Ops:
  7.2 116.6 %copy-start = (bf16[256,1536]{1,0:T(8,128)(2,1)S(1)}, bf16[256,1536]{1,0:T(8,128)(2,1)}, u32[]{:S(2)}) copy-start(bf16[256,1536]{1,0:T(8,128)(2,1)} %param.18) | copy-start | bytes 2359300
  14.2 43.0 %collective-permute-start.1 = (bf16[256,384]{1,0:T(8,128)(2,1)S(1)}, bf16[256,384]{1,0:T(8,128)(2,1)S(1)}, u32[]{:S(2)}, u32[]{:S(2)}) collective-permute-start(bf16[256,384]{1,0:T(8,128)(2,1)S(1)} %bitcast.125), channel_id=1, source_target_pairs={{0,4},{4,8},{8,12},{12,16},{16,20},{20,24},{24,28},{1,5},{5,9},{9,... | collective-permute-start | bytes 589832 | tf_op jit(solution)/shard_map/ppermute | solution.py:13
  20.2 37.0 %collective-permute-start.3 = (bf16[256,384]{1,0:T(8,128)(2,1)S(1)}, bf16[256,384]{1,0:T(8,128)(2,1)S(1)}, u32[]{:S(2)}, u32[]{:S(2)}) collective-permute-start(bf16[256,384]{1,0:T(8,128)(2,1)S(1)} %bitcast.126), channel_id=1, source_target_pairs={{0,8},{4,12},{8,16},{12,20},{16,24},{20,28},{1,9},{5,13},{9,17},{1... | collective-permute-start | bytes 589832 | tf_op jit(solution)/shard_map/ppermute | solution.py:13
  24.8 10.5 %copy-start.1 = (bf16[64,1536]{1,0:T(8,128)(2,1)S(1)}, bf16[64,1536]{1,0:T(8,128)(2,1)}, u32[]{:S(2)}) copy-start(bf16[64,1536]{1,0:T(8,128)(2,1)} %param.14) | copy-start | bytes 589828
  24.8 32.5 %collective-permute-start.5 = (bf16[256,384]{1,0:T(8,128)(2,1)S(1)}, bf16[256,384]{1,0:T(8,128)(2,1)S(1)}, u32[]{:S(2)}, u32[]{:S(2)}) collective-permute-start(bf16[256,384]{1,0:T(8,128)(2,1)S(1)} %bitcast.127), channel_id=1, source_target_pairs={{0,12},{4,16},{8,20},{12,24},{16,28},{1,13},{5,17},{9,21},{13,25},... | collective-permute-start | bytes 589832 | tf_op jit(solution)/shard_map/ppermute | solution.py:13
  30.5 26.8 %collective-permute-start.7 = (bf16[256,384]{1,0:T(8,128)(2,1)S(1)}, bf16[256,384]{1,0:T(8,128)(2,1)S(1)}, u32[]{:S(2)}, u32[]{:S(2)}) collective-permute-start(bf16[256,384]{1,0:T(8,128)(2,1)S(1)} %bitcast.128), channel_id=1, source_target_pairs={{0,16},{4,20},{8,24},{12,28},{1,17},{5,21},{9,25},{13,29},{2,18},{... | collective-permute-start | bytes 589832 | tf_op jit(solution)/shard_map/ppermute | solution.py:13
  32.5 4.0 %collective-permute-start = (bf16[4]{0:T(256)(128)(2,1)S(1)}, bf16[4]{0:T(256)(128)(2,1)S(1)}, u32[]{:S(2)}, u32[]{:S(2)}) collective-permute-start(bf16[4]{0:T(256)(128)(2,1)S(1)} %get-tuple-element.5), channel_id=1, source_target_pairs={{0,4},{4,8},{8,12},{12,16},{16,20},{20,24},{24,28},{1,5},{5,9},{9,... | collective-permute-start | bytes 32 | tf_op jit(solution)/shard_map/ppermute | solution.py:13
  36.5 15.5 %collective-permute-start.6 = (bf16[4]{0:T(256)(128)(2,1)S(1)}, bf16[4]{0:T(256)(128)(2,1)S(1)}, u32[]{:S(2)}, u32[]{:S(2)}) collective-permute-start(bf16[4]{0:T(256)(128)(2,1)S(1)} %get-tuple-element.14), channel_id=1, source_target_pairs={{0,16},{4,20},{8,24},{12,28},{1,17},{5,21},{9,25},{13,29},{2,18},{... | collective-permute-start | bytes 32 | tf_op jit(solution)/shard_map/ppermute | solution.py:13
  52.1 2.6 collective-permute-start.4
  54.6 2.6 collective-permute-start.2
  76.9 5.1 %copy-start.8 = (bf16[1536,256]{1,0:T(8,128)(2,1)S(1)}, bf16[1536,256]{1,0:T(8,128)(2,1)}, u32[]{:S(2)}) copy-start(bf16[1536,256]{1,0:T(8,128)(2,1)} %param.16) | copy-start | bytes 2359300
  76.9 5.5 %copy-start.9 = (bf16[1536,256]{1,0:T(8,128)(2,1)S(1)}, bf16[1536,256]{1,0:T(8,128)(2,1)}, u32[]{:S(2)}) copy-start(bf16[1536,256]{1,0:T(8,128)(2,1)} %param.17) | copy-start | bytes 2359300
  76.9 47.5 %all-to-all-start = ((bf16[4,4,256,384]{3,2,1,0:T(8,128)(2,1)}), bf16[4,4,256,384]{3,2,1,0:T(8,128)(2,1)}, u32[]{:S(2)}, u32[]{:S(2)}) async-start(bf16[4,4,256,384]{3,2,1,0:T(8,128)(2,1)} %stack.2), calls=%async_computation | async-start | bytes 6291456 | tf_op jit(solution)/shard_map/all_to_all | solution.py:87
  81.7 1.2 copy-start.12
  81.7 1.4 copy-start.11
  81.7 91.9 %reduce-scatter.7.cloned.1.call-start = ((), (), s32[]{:S(2)}) async-start(), calls=%async_computation.4 | async-start | bytes 983040
  124.3 12.4 %copy-start.4 = (bf16[4,64,4,64]{3,2,1,0:T(4,128)(2,1)}, bf16[4,64,4,64]{3,2,1,0:T(4,128)(2,1)S(1)}, u32[]{:S(2)}) copy-start(bf16[4,64,4,64]{3,2,1,0:T(4,128)(2,1)S(1)} %reshape.223) | copy-start | bytes 393220
  129.3 1.7 copy-start.2
  132.8 1.1 copy-start.10
  139.7 0.9 copy-start.6
  143.8 108.0 %reduce-scatter.5.cloned.1.call-start = ((), (), s32[]{:S(2)}) async-start(), calls=%async_computation.3 | async-start | bytes 3538944 | tf_op jit(solution)/shard_map/reduce_scatter | solution.py:197
  147.2 1.0 copy-start.5
  147.2 1.5 copy-start.7
  147.3 0.9 copy-start.3
Sparse Core Ops, SparseCore 0:
  143.9 29.6 reduce-scatter.6
  177.2 74.5 reduce-scatter.4
